TPU v7x, 256 devices: a whole 4x4x8 slice. The times are simulated.
256 devices in a mesh: section: 2 (over x_hi), row: 8 (over y, x_lo), col: 16 (over z, core).
Axes of the slice: x: 4 (x_hi: 2, x_lo: 2; x = x_hi * 2 + x_lo), y: 4, z: 8, core: 2. Of those that a mesh axis runs over, the one named last changes fastest.
Arguments:
- images: bfloat16 [2, 8, 48, 128, 256], P('section', None, None, 'row', 'col'), may hold values from -6 to 6
- stem_first: bfloat16 [48, 256], replicated, may hold values from -0.875 to 0.875
- stem_conv: bfloat16 [3, 3, 256, 256], replicated, may hold values from -0.125 to 0.125
- patch_weight: bfloat16 [4096, 1024], P('col'), may hold values from -0.09375 to 0.09375
- position: bfloat16 [64, 32, 1024], P('col', 'row'), may hold values from -6 to 6
- gain_attn: float32 [1024], replicated, may hold values from 0.1 to 1.9
- w_qkv: bfloat16 [3, 1024, 1024], P(None, None, 'col'), may hold values from -0.5 to 0.5
- w_out: bfloat16 [1024, 1024], P('col'), may hold values from -0.1875 to 0.1875
- gain_mlp: float32 [1024], replicated, may hold values from 0.1 to 1.9
- w_up: bfloat16 [1024, 4096], P(None, 'col'), may hold values from -0.1875 to 0.1875
- w_down: bfloat16 [4096, 1024], P('col'), may hold values from -0.09375 to 0.09375
Outputs:
- encoded: bfloat16 [2, 8, 64, 32, 1024], P('section', 'row', 'col')
All inputs are finite; a program needn't handle non-finite values.
Results may differ from a plain program's by a relative error of at most 0.024.
The roundings to bfloat16 on the way count: a program that leaves them out, or rounds other values in their place, can miss the bound.
Values may be sent and summed in bfloat16 or wider, within the bound.
No kernel may reach another device: no remote copies, remote signals or barrier semaphores. Data moves between devices by JAX's collectives and lax.ppermute only.
A program may use at most 64 MiB of HBM per device.

v0:
```python
import math
import jax
import jax.numpy as jnp
from jax import lax
from jax.sharding import PartitionSpec as P

HD = 64


def with_halo(block, sides, width):
    for axis, dim in sides:
        count = lax.axis_size(axis)
        forward = [(i, i + 1) for i in range(count - 1)]
        backward = [(target, source) for source, target in forward]
        low = lax.ppermute(
            lax.slice_in_dim(block, block.shape[dim] - width, None, axis=dim), axis, forward
        )
        high = lax.ppermute(lax.slice_in_dim(block, 0, width, axis=dim), axis, backward)
        block = jnp.concatenate([low, block, high], axis=dim)
    return block


def passed_along(value, axis, steps):
    count = lax.axis_size(axis)
    pairs = [(source, (source + steps) % count) for source in range(count)]
    return lax.ppermute(value, axis, pairs)


def layer_norm(vectors, gain_vec):
    row_mean = jnp.mean(vectors, axis=-1, keepdims=True)
    center = vectors - row_mean
    spread = jnp.mean(center * center, axis=-1, keepdims=True)
    return center * lax.rsqrt(spread + 1e-06) * gain_vec


def stem_features(images, stem_first, stem_conv):
    pixels = images[0]
    first_map = jnp.einsum("ikhw,kc->ihwc", pixels, stem_first, preferred_element_type=jnp.float32)
    stem_maps = jnp.maximum(first_map, 0.0).astype(jnp.bfloat16)
    padded = with_halo(stem_maps, (("row", 1), ("col", 2)), 1)
    img_count, height, tile_width, channels = stem_maps.shape
    summed = stem_maps.astype(jnp.float32)
    for offset_a in range(3):
        for offset_b in range(3):
            window = padded[:, offset_a : offset_a + height, offset_b : offset_b + tile_width, :]
            summed = summed + jnp.einsum(
                "ihwc,cd->ihwd",
                window,
                stem_conv[offset_a, offset_b],
                preferred_element_type=jnp.float32,
            )
    deep_maps = jnp.maximum(summed, 0.0).astype(jnp.bfloat16)
    blocks = deep_maps.reshape(img_count, height // 4, 4, tile_width // 4, 4, channels).transpose(
        0, 3, 1, 2, 4, 5
    )
    return blocks.reshape(img_count, tile_width // 4, height // 4, 16 * channels)


def on_device(
    images,
    stem_first,
    stem_conv,
    patch_weight,
    position,
    gain_attn,
    w_qkv,
    w_out,
    gain_mlp,
    w_up,
    w_down,
):
    features = stem_features(images, stem_first, stem_conv)
    img_count, cols_here, rows_here, feat_width = features.shape
    model_width = patch_weight.shape[1]
    flat_local = features.reshape(-1, feat_width)
    embedded = jnp.dot(
        flat_local,
        lax.all_gather(patch_weight, "col", axis=0, tiled=True),
        preferred_element_type=jnp.float32,
    )
    local_tokens = (
        embedded.reshape(img_count, cols_here, rows_here, model_width)
        + position.astype(jnp.float32)[None]
    ).astype(jnp.bfloat16)
    arrived = passed_along(local_tokens, "section", 1)
    token_image = lax.all_to_all(arrived, "row", split_axis=0, concat_axis=2, tiled=True)
    tokens_in = token_image.reshape(-1, model_width)
    residual = tokens_in.astype(jnp.float32)
    normed = layer_norm(residual, gain_attn).astype(jnp.bfloat16)
    projected = jnp.einsum(
        "td,kdh->kth",
        lax.all_gather(normed, "col", axis=0, tiled=True),
        w_qkv,
        preferred_element_type=jnp.float32,
    ).astype(jnp.bfloat16)
    token_count = projected.shape[1]
    local_heads = w_out.shape[0] // HD
    split_heads = projected.reshape(3, token_count, local_heads, HD).transpose(0, 2, 1, 3)
    key_heads = split_heads[1]
    value_heads = split_heads[2]
    block_rows = math.gcd(token_count, 512)
    query_blocks = (
        split_heads[0]
        .reshape(local_heads, token_count // block_rows, block_rows, HD)
        .transpose(1, 0, 2, 3)
    )

    def attend(query_block):
        scores = jnp.einsum(
            "hqd,hkd->hqk", query_block, key_heads, preferred_element_type=jnp.float32
        ) * HD ** (-0.5)
        row_peak = jnp.max(scores, axis=-1, keepdims=True)
        expo = jnp.exp(scores - row_peak)
        prob_rows = (expo / jnp.sum(expo, axis=-1, keepdims=True)).astype(jnp.bfloat16)
        return jnp.einsum(
            "hqk,hkd->hqd", prob_rows, value_heads, preferred_element_type=jnp.float32
        ).astype(jnp.bfloat16)

    attended = lax.map(attend, query_blocks)
    mixed_heads = attended.transpose(0, 2, 1, 3).reshape(token_count, local_heads * HD)
    row_slice = mixed_heads
    after = residual + lax.psum_scatter(
        jnp.dot(row_slice, w_out, preferred_element_type=jnp.float32).astype(jnp.bfloat16),
        "col",
        scatter_dimension=0,
        tiled=True,
    ).astype(jnp.float32)
    normed_mlp = layer_norm(after, gain_mlp).astype(jnp.bfloat16)
    hidden = jax.nn.gelu(
        jnp.dot(
            lax.all_gather(normed_mlp, "col", axis=0, tiled=True),
            w_up,
            preferred_element_type=jnp.float32,
        ),
        approximate=True,
    ).astype(jnp.bfloat16)
    row_slice = hidden
    encoded = (
        after
        + lax.psum_scatter(
            jnp.dot(row_slice, w_down, preferred_element_type=jnp.float32).astype(jnp.bfloat16),
            "col",
            scatter_dimension=0,
            tiled=True,
        ).astype(jnp.float32)
    ).astype(jnp.bfloat16)
    return encoded.reshape(1, 1, cols_here, -1, model_width)


def solution(mesh):
    placed = (
        P("section", None, None, "row", "col"),
        P(),
        P(),
        P("col", None),
        P("col", "row", None),
        P(),
        P(None, None, "col"),
        P("col", None),
        P(),
        P(None, "col"),
        P("col", None),
    )
    return jax.shard_map(
        on_device,
        mesh=mesh,
        in_specs=placed,
        out_specs=P("section", "row", "col", None, None),
        check_vma=False,
    )
```

profile of v0, /device:TPU:2, one launch (start us, length us, event | category | flops | bytes accessed | tf_op | source)
XLA Modules:
  0.0 342.6 jit_solution(3398416995939762517)
XLA Ops:
  6.5 0.7 all-gather.4.cloned.1.call-update
  7.3 1.4 maximum_convert_fusion.1
  8.8 3.5 %collective-permute-start = (bf16[8,1,16,256]{3,2,1,0:T(8,128)(2,1)S(1)}, bf16[8,1,16,256]{3,2,1,0:T(8,128)(2,1)S(1)}, u32[]{:S(2)}, u32[]{:S(2)}) collective-permute-start(bf16[8,1,16,256]{3,2,1,0:T(8,128)(2,1)S(1)} %get-tuple-element.64), channel_id=1, source_target_pairs={{0,16},{16,32},{32,48},{48,64},{64,80},{80,96},{96,112},{1,17},{17... | collective-permute-start | bytes 196616 | tf_op jit(solution)/shard_map/ppermute | solution.py:15
  12.3 2.4 collective-permute-start.1
  14.7 0.4 fusion.61
  15.1 4.2 %collective-permute-done.1 = bf16[8,1,16,256]{3,2,1,0:T(8,128)(2,1)S(1)} collective-permute-done((bf16[8,1,16,256]{3,2,1,0:T(8,128)(2,1)S(1)}, bf16[8,1,16,256]{3,2,1,0:T(8,128)(2,1)S(1)}, u32[]{:S(2)}, u32[]{:S(2)}) %collective-permute-start.1) | collective-permute-done | bytes 65568 | tf_op jit(solution)/shard_map/ppermute | solution.py:18
  19.6 1.3 collective-permute-start.2
  20.9 1.3 collective-permute-start.3
  22.2 0.4 fusion.28
  22.6 0.4 fusion.32
  23.0 3.2 collective-permute-done.3
  26.3 1.2 pad_maximum_fusion
  27.4 0.4 fusion.41
  28.3 0.5 fusion.43
  28.8 0.5 fusion.47
  29.2 0.4 fusion.49
  29.7 1.2 maximum_convert_fusion
  31.1 1.1 copy.24
  32.3 35.9 %all-gather.4.cloned.1.call-done = bf16[4096,1024]{1,0:T(8,128)(2,1)} async-done(((bf16[256,1024]{1,0:T(8,128)(2,1)}), bf16[4096,1024]{1,0:T(8,128)(2,1)}) %all-gather.4.cloned.1.call-update) | async-done | bytes 8388624 | tf_op jit(solution)/shard_map/all_gather | solution.py:78
  68.2 4.6 %fusion.25 = bf16[8,4,4,1024]{3,0,2,1:T(8,128)(2,1)S(1)} fusion(bf16[8,4,4,4096]{3,0,2,1:T(8,128)(2,1)S(1)} %bitcast.143, bf16[4096,1024]{1,0:T(8,128)(2,1)} %all-gather.4.cloned.1.call-done, f32[4,4,1024]{2,1,0:T(4,128)S(1)} %convert_element_type.74), kind=kOutput, calls=%fused_computation.33 | convolution fusion | flops 1074003968 | bytes 9764864 | tf_op jit(solution)/shard_map/dot_general | solution.py:76
  72.8 2.2 collective-permute-start.4
  75.0 7.9 %collective-permute-done.4 = bf16[8,4,4,1024]{3,0,2,1:T(8,128)(2,1)S(1)} collective-permute-done((bf16[8,4,4,1024]{3,0,2,1:T(8,128)(2,1)S(1)}, bf16[8,4,4,1024]{3,0,2,1:T(8,128)(2,1)S(1)}, u32[]{:S(2)}, u32[]{:S(2)}) %collective-permute-start.4) | collective-permute-done | bytes 262176 | tf_op jit(solution)/shard_map/ppermute | solution.py:26
  83.1 11.7 %all_to_all.4 = bf16[8,4,4,1024]{3,2,1,0:T(4,128)(2,1)S(1)} all-to-all(bf16[8,4,4,1024]{3,2,1,0:T(4,128)(2,1)S(1)} %copy.25), channel_id=1, replica_groups=mesh['section'=2,'row'=8,'col'=16] {'row'}, dimensions={0} | all-to-all | bytes 524288 | tf_op jit(solution)/shard_map/all_to_all | solution.py:86
  96.3 0.8 multiply_convert_fusion.1
  97.4 40.1 %all-gather.6.cloned.1.call-done = bf16[2048,1024]{1,0:T(8,128)(2,1)} async-done(((bf16[128,1024]{1,0:T(8,128)(2,1)}), bf16[2048,1024]{1,0:T(8,128)(2,1)}) %all-gather.6.cloned.1.call-update) | async-done | bytes 4194320 | tf_op jit(solution)/shard_map/all_gather | solution.py:92
  137.6 3.7 %fusion.88 = f32[2048,192]{0,1:S(1)} fusion(bf16[2048,1024]{1,0:T(8,128)(2,1)} %all-gather.6.cloned.1.call-done, bf16[1024,192]{0,1:T(8,128)(2,1)S(1)} %bitcast.148), kind=kOutput, calls=%fused_computation.105 | convolution fusion | flops 805306368 | bytes 6160384
  142.3 11.1 %while.10 = (s32[]{:T(128)}, bf16[4,1,512,64]{2,3,1,0:T(8,128)(2,1)S(1)}, bf16[4,1,512,64]{3,2,1,0:T(8,128)(2,1)S(1)}, bf16[1,2048,64]{2,1,0:T(8,128)(2,1)S(1)}, bf16[1,2048,64]{2,1,0:T(8,128)(2,1)S(1)}, /*index=5*/s32[]{:T(128)}) while((s32[]{:T(128)}, bf16[4,1,512,64]{2,3,1,0:T(8,128)(2,1)S(1)}, bf16[4,1,512,64]{3,2,1,0:T(8,128)(2,1)S(1)}, ...), condition=%wide.region_5.6_spmd, body=%wide.region_2.5_spmd.sunk | while | flops 277904384 | bytes 13838413 | solution.py:119
  142.4 0.8 multiply_reduce_fusion.4
  143.1 0.8 fusion.102
  144.0 1.1 fusion.103
  145.1 0.8 multiply_reduce_fusion.4
  145.9 0.8 fusion.102
  146.8 1.1 fusion.103
  147.9 0.8 multiply_reduce_fusion.4
  148.7 0.8 fusion.102
  149.5 1.1 fusion.103
  150.7 0.8 multiply_reduce_fusion.4
  151.5 0.8 fusion.102
  152.3 1.1 fusion.103
  153.8 3.2 convolution_convert_fusion.1
  157.1 61.9 %reduce-scatter.3.cloned.1.call-done = bf16[128,1024]{1,0:T(8,128)(2,1)} async-done(((bf16[2048,1024]{1,0:T(8,128)(2,1)}), bf16[128,1024]{1,0:T(8,128)(2,1)}) %reduce-scatter.3.cloned.1.call-update) | async-done | bytes 262160 | tf_op jit(solution)/shard_map/reduce_scatter | solution.py:122
  219.0 1.1 fusion.76
  220.1 1.1 multiply_reduce_fusion.1
  221.2 1.8 multiply_convert_fusion
  223.1 40.5 %all-gather.8.cloned.1.call-done = bf16[2048,1024]{1,0:T(8,128)(2,1)} async-done(((bf16[128,1024]{1,0:T(8,128)(2,1)}), bf16[2048,1024]{1,0:T(8,128)(2,1)}) %all-gather.8.cloned.1.call-update) | async-done | bytes 4194320 | tf_op jit(solution)/shard_map/all_gather | solution.py:131
  263.6 8.5 %convolution_convert_fusion = bf16[2048,1024]{1,0:T(8,128)(2,1)} fusion(bf16[256,1024]{1,0:T(8,128)(2,1)S(1)} %copy-done, bf16[2048,1024]{1,0:T(8,128)(2,1)} %all-gather.8.cloned.1.call-done, bf16[1024,256]{1,0:T(8,128)(2,1)S(1)} %copy-done.8), kind=kOutput, calls=%fused_computation.17 | convolution fusion | flops 2154299392 | bytes 9437184 | tf_op jit(solution)/shard_map/dot_general | solution.py:141
  272.1 62.1 %reduce-scatter.5.cloned.1.call-done = bf16[128,1024]{1,0:T(8,128)(2,1)} async-done(((bf16[2048,1024]{1,0:T(8,128)(2,1)}), bf16[128,1024]{1,0:T(8,128)(2,1)}) %reduce-scatter.5.cloned.1.call-update) | async-done | bytes 262160 | tf_op jit(solution)/shard_map/reduce_scatter | solution.py:140
  334.3 1.7 add_convert_fusion
  (59 shorter events, 4.4 us)
Async XLA Ops:
  6.5 257.1 %copy-start = (bf16[256,1024]{1,0:T(8,128)(2,1)S(1)}, bf16[256,1024]{1,0:T(8,128)(2,1)}, u32[]{:S(2)}) copy-start(bf16[256,1024]{1,0:T(8,128)(2,1)} %param.23) | copy-start | bytes 1572868
  6.5 8.1 %copy-start.2 = (bf16[3,3,256,256]{3,2,1,0:T(8,128)(2,1)S(1)}, bf16[3,3,256,256]{3,2,1,0:T(8,128)(2,1)}, u32[]{:S(2)}) copy-start(bf16[3,3,256,256]{3,2,1,0:T(8,128)(2,1)} %param.15) | copy-start | bytes 3538948
  6.5 61.7 %all-gather.4.cloned.1.call-start = ((), (), s32[]{:S(2)}) async-start(), calls=%async_computation.3 | async-start | bytes 8912896 | tf_op jit(solution)/shard_map/all_gather | solution.py:78
  7.3 130.3 %all-gather.6.cloned.1.call-start = ((), (), s32[]{:S(2)}) async-start(), calls=%async_computation.4 | async-start | bytes 4456448 | tf_op jit(solution)/shard_map/all_gather | solution.py:92
  8.8 6.3 %copy-start.5 = (bf16[4,4,1024]{2,1,0:T(4,128)(2,1)S(1)}, bf16[4,4,1024]{2,1,0:T(4,128)(2,1)}, u32[]{:S(2)}) copy-start(bf16[4,4,1024]{2,1,0:T(4,128)(2,1)} %param.17) | copy-start | bytes 98308
  8.8 6.3 %collective-permute-start = (bf16[8,1,16,256]{3,2,1,0:T(8,128)(2,1)S(1)}, bf16[8,1,16,256]{3,2,1,0:T(8,128)(2,1)S(1)}, u32[]{:S(2)}, u32[]{:S(2)}) collective-permute-start(bf16[8,1,16,256]{3,2,1,0:T(8,128)(2,1)S(1)} %get-tuple-element.64), channel_id=1, source_target_pairs={{0,16},{16,32},{32,48},{48,64},{64,80},{80,96},{96,112},{1,17},{17... | collective-permute-start | bytes 196616 | tf_op jit(solution)/shard_map/ppermute | solution.py:15
  12.3 7.1 %collective-permute-start.1 = (bf16[8,1,16,256]{3,2,1,0:T(8,128)(2,1)S(1)}, bf16[8,1,16,256]{3,2,1,0:T(8,128)(2,1)S(1)}, u32[]{:S(2)}, u32[]{:S(2)}) collective-permute-start(bf16[8,1,16,256]{3,2,1,0:T(8,128)(2,1)S(1)} %get-tuple-element.65), channel_id=1, source_target_pairs={{16,0},{32,16},{48,32},{64,48},{80,64},{96,80},{112,96},{17,1},{33... | collective-permute-start | bytes 196616 | tf_op jit(solution)/shard_map/ppermute | solution.py:18
  19.6 3.5 %collective-permute-start.2 = (bf16[8,18,1,256]{3,2,1,0:T(2,128)(2,1)S(1)}, bf16[8,18,1,256]{3,2,1,0:T(2,128)(2,1)S(1)}, u32[]{:S(2)}, u32[]{:S(2)}) collective-permute-start(bf16[8,18,1,256]{3,2,1,0:T(2,128)(2,1)S(1)} %get-tuple-element.63), channel_id=1, source_target_pairs={{0,1},{1,2},{2,3},{3,4},{4,5},{5,6},{6,7},{7,8},{8,9},{9,10},{10,1... | collective-permute-start | bytes 221192 | tf_op jit(solution)/shard_map/ppermute | solution.py:15
  20.9 5.4 %collective-permute-start.3 = (bf16[8,18,1,256]{3,2,1,0:T(2,128)(2,1)S(1)}, bf16[8,18,1,256]{3,2,1,0:T(2,128)(2,1)S(1)}, u32[]{:S(2)}, u32[]{:S(2)}) collective-permute-start(bf16[8,18,1,256]{3,2,1,0:T(2,128)(2,1)S(1)} %get-tuple-element.62), channel_id=1, source_target_pairs={{1,0},{2,1},{3,2},{4,3},{5,4},{6,5},{7,6},{8,7},{9,8},{10,9},{11,1... | collective-permute-start | bytes 221192 | tf_op jit(solution)/shard_map/ppermute | solution.py:18
  72.8 10.0 %collective-permute-start.4 = (bf16[8,4,4,1024]{3,0,2,1:T(8,128)(2,1)S(1)}, bf16[8,4,4,1024]{3,0,2,1:T(8,128)(2,1)S(1)}, u32[]{:S(2)}, u32[]{:S(2)}) collective-permute-start(bf16[8,4,4,1024]{3,0,2,1:T(8,128)(2,1)S(1)} %fusion.25), channel_id=1, source_target_pairs={{0,128},{128,0},{1,129},{129,1},{2,130},{130,2},{3,131},{131,3},{4... | collective-permute-start | bytes 786440 | tf_op jit(solution)/shard_map/ppermute | solution.py:26
  83.1 13.2 %copy-start.6 = (f32[1024]{0:T(1024)S(1)}, f32[1024]{0:T(1024)}, u32[]{:S(2)}) copy-start(f32[1024]{0:T(1024)} %param.18) | copy-start | bytes 12292
  95.3 42.3 %copy-start.3 = (bf16[3,1024,64]{1,2,0:T(8,128)(2,1)S(1)}, bf16[3,1024,64]{1,2,0:T(8,128)(2,1)}, u32[]{:S(2)}) copy-start(bf16[3,1024,64]{1,2,0:T(8,128)(2,1)} %param.19) | copy-start | bytes 1179652
  97.2 121.8 %reduce-scatter.3.cloned.1.call-start = ((), (), s32[]{:S(2)}) async-start(), calls=%async_computation.5 | async-start | bytes 4456448 | tf_op jit(solution)/shard_map/reduce_scatter | solution.py:122
  142.3 11.4 %copy-start.4 = (bf16[64,1024]{1,0:T(8,128)(2,1)S(1)}, bf16[64,1024]{1,0:T(8,128)(2,1)}, u32[]{:S(2)}) copy-start(bf16[64,1024]{1,0:T(8,128)(2,1)} %param.20) | copy-start | bytes 393220
  157.0 64.2 %copy-start.7 = (f32[1024]{0:T(1024)S(1)}, f32[1024]{0:T(1024)}, u32[]{:S(2)}) copy-start(f32[1024]{0:T(1024)} %param.21) | copy-start | bytes 12292
  157.0 106.6 %copy-start.8 = (bf16[1024,256]{1,0:T(8,128)(2,1)S(1)}, bf16[1024,256]{1,0:T(8,128)(2,1)}, u32[]{:S(2)}) copy-start(bf16[1024,256]{1,0:T(8,128)(2,1)} %param.22) | copy-start | bytes 1572868
  157.0 106.6 %all-gather.8.cloned.1.call-start = ((), (), s32[]{:S(2)}) async-start(), calls=%async_computation.6 | async-start | bytes 4456448 | tf_op jit(solution)/shard_map/all_gather | solution.py:131
  223.1 111.2 %reduce-scatter.5.cloned.1.call-start = ((), (), s32[]{:S(2)}) async-start(), calls=%async_computation.7 | async-start | bytes 4456448 | tf_op jit(solution)/shard_map/reduce_scatter | solution.py:140
  272.1 62.2 %copy-start.1 = (bf16[128,1024]{1,0:T(8,128)(2,1)S(1)}, bf16[128,1024]{1,0:T(8,128)(2,1)}, u32[]{:S(2)}) copy-start(bf16[128,1024]{1,0:T(8,128)(2,1)} %reduce-scatter.3.cloned.1.call-done) | copy-start | bytes 786436
Sparse Core Ops, SparseCore 0:
  9.2 58.9 all-gather.3
  97.3 40.1 all-gather.5
  157.1 61.7 reduce-scatter.2
  223.2 40.3 all-gather.7
  272.3 61.9 reduce-scatter.4
where the time goes:
time: 343 us
  waiting for transfers between devices  257 us (75%)
  matrix products  34 us (10%)
  between operations  13.4 us (4%)
  other arithmetic  12 us (3%)
  blocking collectives  11.7 us (3%)
  starting transfers between devices  10.9 us (3%)
  local copies, waits for them, and re-layouts  3.78 us (1%)
    reduce_scatter x1, waiting for transfers between devices, on_device(): lax.psum_scatter(jnp.dot(row_slice, w_down, preferred_element_type=jnp.fl...  62.1 us
    reduce_scatter x1, waiting for transfers between devices, on_device(): lax.psum_scatter(jnp.dot(row_slice, w_out, preferred_element_type=jnp.flo...  61.9 us
    all_gather x1, waiting for transfers between devices, on_device(): lax.all_gather(normed_mlp, 'col', axis=0, tiled=True)  40.5 us
    all_gather x1, waiting for transfers between devices, on_device(): lax.all_gather(normed, 'col', axis=0, tiled=True)  40.1 us
    all_gather x1, waiting for transfers between devices, on_device(): lax.all_gather(patch_weight, 'col', axis=0, tiled=True)  35.9 us
    all_to_all x1, blocking collectives, on_device(): lax.all_to_all(arrived, 'row', split_axis=0, concat_axis=2, tiled=True)  11.7 us
    dot_general x1, matrix products, on_device(): jnp.dot(row_slice, w_down, preferred_element_type=jnp.float32)  8.49 us
    ppermute x1, waiting for transfers between devices, passed_along(): return lax.ppermute(value, axis, pairs)  7.88 us
  transfers between devices with their start and end apart: 10, of which 8 were waited for; matrix products, arithmetic and copies ran while one was open for 3% of the time, Pallas kernels for 0%

commit v1 on v0

--- a/solution.py
+++ b/solution.py
@@ -75,7 +75,9 @@
     flat_local = features.reshape(-1, feat_width)
     embedded = jnp.dot(
         flat_local,
-        lax.all_gather(patch_weight, "col", axis=0, tiled=True),
+        jnp.concatenate(
+            lax.all_to_all(jnp.stack([patch_weight] * lax.axis_size("col")), "col", 0, 0), axis=0
+        ),
         preferred_element_type=jnp.float32,
     )
     local_tokens = (

time: 343 us -> 486 us (1.42)
  waiting for transfers between devices: 257 us -> 386 us
  starting transfers between devices: 10.9 us -> 19.7 us
  local copies, waits for them, and re-layouts: 3.78 us -> 9.19 us
    all_to_all x0 -> x1, waiting for transfers between devices: none -> 160 us  [on_device(): lax.all_to_all(jnp.stack([patch_weight] * lax.axis_size('col')), 'col', 0...]
    all_gather x1 -> x0, waiting for transfers between devices: 35.9 us -> none  [on_device(): lax.all_gather(patch_weight, 'col', axis=0, tiled=True)]
    all_to_all x0 -> x1, starting transfers between devices: none -> 8.75 us  [on_device(): lax.all_to_all(jnp.stack([patch_weight] * lax.axis_size('col')), 'col', 0...]
    all_gather x1, waiting for transfers between devices: 40.1 us -> 48.4 us  [on_device(): lax.all_gather(normed, 'col', axis=0, tiled=True)]
    another operation x0 -> x1, local copies, waits for them, and re-layouts: none -> 5.41 us  [on_device(): jnp.stack([patch_weight] * lax.axis_size('col'))]
  transfers between devices with their start and end apart: 10 -> 10, of which waited for: 8 -> 8; matrix products, arithmetic and copies ran while one was open for 3% -> 2% of each run, Pallas kernels for 0% -> 0%
where the time goes in v1:
time: 486 us
  waiting for transfers between devices  386 us (79%)
  matrix products  32.9 us (7%)
  starting transfers between devices  19.7 us (4%)
  between operations  13.5 us (3%)
  other arithmetic  12 us (2%)
  blocking collectives  11.8 us (2%)
  local copies, waits for them, and re-layouts  9.19 us (2%)
    all_to_all x1, waiting for transfers between devices, on_device(): lax.all_to_all(jnp.stack([patch_weight] * lax.axis_size('col')), 'col', 0...  160 us
    reduce_scatter x1, waiting for transfers between devices, on_device(): lax.psum_scatter(jnp.dot(row_slice, w_down, preferred_element_type=jnp.fl...  62 us
    reduce_scatter x1, waiting for transfers between devices, on_device(): lax.psum_scatter(jnp.dot(row_slice, w_out, preferred_element_type=jnp.flo...  61.9 us
    all_gather x1, waiting for transfers between devices, on_device(): lax.all_gather(normed, 'col', axis=0, tiled=True)  48.4 us
    all_gather x1, waiting for transfers between devices, on_device(): lax.all_gather(normed_mlp, 'col', axis=0, tiled=True)  40.7 us
    all_to_all x1, blocking collectives, on_device(): lax.all_to_all(arrived, 'row', split_axis=0, concat_axis=2, tiled=True)  11.8 us
  transfers between devices with their start and end apart: 10, of which 8 were waited for; matrix products, arithmetic and copies ran while one was open for 2% of the time, Pallas kernels for 0%

profile of v1, /device:TPU:2, one launch (start us, length us, event | category | flops | bytes accessed | tf_op | source)
XLA Modules:
  0.0 485.7 jit_solution(3135001879385161445)
XLA Ops:
  6.5 5.4 %stack.2 = bf16[16,256,1024]{2,1,0:T(8,128)(2,1)} broadcast(bf16[256,1024]{1,0:T(8,128)(2,1)} %param.16), dimensions={1,2} | broadcast | bytes 8912896 | tf_op jit(solution)/shard_map/stack | solution.py:79
  12.0 8.8 %all-to-all-start = ((bf16[16,256,1024]{2,1,0:T(8,128)(2,1)}), bf16[16,256,1024]{2,1,0:T(8,128)(2,1)}, u32[]{:S(2)}, u32[]{:S(2)}) async-start(bf16[16,256,1024]{2,1,0:T(8,128)(2,1)} %stack.2), calls=%async_computation | async-start | bytes 16777216 | tf_op jit(solution)/shard_map/all_to_all | solution.py:79
  21.2 3.5 collective-permute-start
  24.7 2.4 collective-permute-start.1
  27.1 0.4 fusion.54
  27.6 4.2 collective-permute-done.1
  32.0 1.3 collective-permute-start.2
  33.3 1.3 collective-permute-start.3
  34.6 0.4 fusion.21
  35.0 0.4 fusion.25
  35.5 3.2 collective-permute-done.3
  38.7 1.2 pad_maximum_fusion
  40.3 0.4 fusion.38
  40.7 0.5 fusion.36
  41.1 0.5 fusion.40
  41.6 0.4 fusion.42
  42.0 1.2 maximum_convert_fusion
  43.5 1.1 copy.24
  44.7 160.3 %all-to-all-done = bf16[16,256,1024]{2,1,0:T(8,128)(2,1)} async-done(((bf16[16,256,1024]{2,1,0:T(8,128)(2,1)}), bf16[16,256,1024]{2,1,0:T(8,128)(2,1)}, u32[]{:S(2)}, u32[]{:S(2)}) %all-to-all-start) | async-done | bytes 8388640 | tf_op jit(solution)/shard_map/all_to_all | solution.py:79
  204.9 4.6 fusion.20
  209.6 2.2 collective-permute-start.4
  211.8 5.8 %collective-permute-done.4 = bf16[8,4,4,1024]{3,0,2,1:T(8,128)(2,1)S(1)} collective-permute-done((bf16[8,4,4,1024]{3,0,2,1:T(8,128)(2,1)S(1)}, bf16[8,4,4,1024]{3,0,2,1:T(8,128)(2,1)S(1)}, u32[]{:S(2)}, u32[]{:S(2)}) %collective-permute-start.4) | collective-permute-done | bytes 262176 | tf_op jit(solution)/shard_map/ppermute | solution.py:26
  217.8 11.8 %all_to_all.14 = bf16[8,4,4,1024]{3,2,1,0:T(4,128)(2,1)S(1)} all-to-all(bf16[8,4,4,1024]{3,2,1,0:T(4,128)(2,1)S(1)} %copy.25), channel_id=1, replica_groups=mesh['section'=2,'row'=8,'col'=16] {'row'}, dimensions={0} | all-to-all | bytes 524288 | tf_op jit(solution)/shard_map/all_to_all | solution.py:88
  231.2 0.8 multiply_convert_fusion.1
  232.3 48.4 %all-gather.3.cloned.1.call-done = bf16[2048,1024]{1,0:T(8,128)(2,1)} async-done(((bf16[128,1024]{1,0:T(8,128)(2,1)}), bf16[2048,1024]{1,0:T(8,128)(2,1)}) %all-gather.3.cloned.1.call-update) | async-done | bytes 4194320 | tf_op jit(solution)/shard_map/all_gather | solution.py:94
  280.7 3.7 fusion.81
  285.5 11.1 %while.10 = (s32[]{:T(128)}, bf16[4,1,512,64]{2,3,1,0:T(8,128)(2,1)S(1)}, bf16[4,1,512,64]{3,2,1,0:T(8,128)(2,1)S(1)}, bf16[1,2048,64]{2,1,0:T(8,128)(2,1)S(1)}, bf16[1,2048,64]{2,1,0:T(8,128)(2,1)S(1)}, /*index=5*/s32[]{:T(128)}) while((s32[]{:T(128)}, bf16[4,1,512,64]{2,3,1,0:T(8,128)(2,1)S(1)}, bf16[4,1,512,64]{3,2,1,0:T(8,128)(2,1)S(1)}, ...), condition=%wide.region_5.6_spmd, body=%wide.region_2.5_spmd.sunk | while | flops 277904384 | bytes 13838413 | solution.py:121
  285.5 0.8 multiply_reduce_fusion.4
  286.3 0.8 fusion.96
  287.1 1.1 fusion.97
  288.3 0.8 multiply_reduce_fusion.4
  289.1 0.8 fusion.96
  289.9 1.1 fusion.97
  291.1 0.8 multiply_reduce_fusion.4
  291.9 0.8 fusion.96
  292.7 1.1 fusion.97
  293.8 0.8 multiply_reduce_fusion.4
  294.6 0.8 fusion.96
  295.5 1.1 fusion.97
  296.9 3.2 convolution_convert_fusion.1
  300.2 61.9 %reduce-scatter.3.cloned.1.call-done = bf16[128,1024]{1,0:T(8,128)(2,1)} async-done(((bf16[2048,1024]{1,0:T(8,128)(2,1)}), bf16[128,1024]{1,0:T(8,128)(2,1)}) %reduce-scatter.3.cloned.1.call-update) | async-done | bytes 262160 | tf_op jit(solution)/shard_map/reduce_scatter | solution.py:124
  362.1 1.1 fusion.69
  363.2 1.1 multiply_reduce_fusion.1
  364.4 1.8 multiply_convert_fusion
  366.2 40.7 %all-gather.5.cloned.1.call-done = bf16[2048,1024]{1,0:T(8,128)(2,1)} async-done(((bf16[128,1024]{1,0:T(8,128)(2,1)}), bf16[2048,1024]{1,0:T(8,128)(2,1)}) %all-gather.5.cloned.1.call-update) | async-done | bytes 4194320 | tf_op jit(solution)/shard_map/all_gather | solution.py:133
  407.0 8.5 %convolution_convert_fusion = bf16[2048,1024]{1,0:T(8,128)(2,1)} fusion(bf16[256,1024]{1,0:T(8,128)(2,1)S(1)} %copy-done, bf16[2048,1024]{1,0:T(8,128)(2,1)} %all-gather.5.cloned.1.call-done, bf16[1024,256]{1,0:T(8,128)(2,1)S(1)} %copy-done.10), kind=kOutput, calls=%fused_computation.15 | convolution fusion | flops 2154299392 | bytes 9437184 | tf_op jit(solution)/shard_map/dot_general | solution.py:143
  415.5 62.0 %reduce-scatter.5.cloned.1.call-done = bf16[128,1024]{1,0:T(8,128)(2,1)} async-done(((bf16[2048,1024]{1,0:T(8,128)(2,1)}), bf16[128,1024]{1,0:T(8,128)(2,1)}) %reduce-scatter.5.cloned.1.call-update) | async-done | bytes 262160 | tf_op jit(solution)/shard_map/reduce_scatter | solution.py:142
  477.4 1.7 add_convert_fusion
  (63 shorter events, 4.8 us)
Async XLA Ops:
  6.5 400.4 %copy-start = (bf16[256,1024]{1,0:T(8,128)(2,1)S(1)}, bf16[256,1024]{1,0:T(8,128)(2,1)}, u32[]{:S(2)}) copy-start(bf16[256,1024]{1,0:T(8,128)(2,1)} %param.23) | copy-start | bytes 1572868
  11.9 8.8 %copy-start.3 = (bf16[1,8,48,16,16]{2,4,3,1,0:T(8,128)(2,1)S(1)}, bf16[1,8,48,16,16]{2,4,3,1,0:T(8,128)(2,1)}, u32[]{:S(2)}) copy-start(bf16[1,8,48,16,16]{2,4,3,1,0:T(8,128)(2,1)} %param.13) | copy-start | bytes 589828
  11.9 8.8 %copy-start.7 = (bf16[48,256]{1,0:T(8,128)(2,1)S(1)}, bf16[48,256]{1,0:T(8,128)(2,1)}, u32[]{:S(2)}) copy-start(bf16[48,256]{1,0:T(8,128)(2,1)} %param.14) | copy-start | bytes 73732
  12.0 15.1 %copy-start.2 = (bf16[3,3,256,256]{3,2,1,0:T(8,128)(2,1)S(1)}, bf16[3,3,256,256]{3,2,1,0:T(8,128)(2,1)}, u32[]{:S(2)}) copy-start(bf16[3,3,256,256]{3,2,1,0:T(8,128)(2,1)} %param.15) | copy-start | bytes 3538948
  12.0 193.0 %all-to-all-start = ((bf16[16,256,1024]{2,1,0:T(8,128)(2,1)}), bf16[16,256,1024]{2,1,0:T(8,128)(2,1)}, u32[]{:S(2)}, u32[]{:S(2)}) async-start(bf16[16,256,1024]{2,1,0:T(8,128)(2,1)} %stack.2), calls=%async_computation | async-start | bytes 16777216 | tf_op jit(solution)/shard_map/all_to_all | solution.py:79
  20.7 260.0 %all-gather.3.cloned.1.call-start = ((), (), s32[]{:S(2)}) async-start(), calls=%async_computation.4 | async-start | bytes 4456448 | tf_op jit(solution)/shard_map/all_gather | solution.py:94
  21.2 6.3 %copy-start.6 = (bf16[4,4,1024]{2,1,0:T(4,128)(2,1)S(1)}, bf16[4,4,1024]{2,1,0:T(4,128)(2,1)}, u32[]{:S(2)}) copy-start(bf16[4,4,1024]{2,1,0:T(4,128)(2,1)} %param.17) | copy-start | bytes 98308
  21.2 6.3 %collective-permute-start = (bf16[8,1,16,256]{3,2,1,0:T(8,128)(2,1)S(1)}, bf16[8,1,16,256]{3,2,1,0:T(8,128)(2,1)S(1)}, u32[]{:S(2)}, u32[]{:S(2)}) collective-permute-start(bf16[8,1,16,256]{3,2,1,0:T(8,128)(2,1)S(1)} %get-tuple-element.64), channel_id=1, source_target_pairs={{0,16},{16,32},{32,48},{48,64},{64,80},{80,96},{96,112},{1,17},{17... | collective-permute-start | bytes 196616 | tf_op jit(solution)/shard_map/ppermute | solution.py:15
  24.7 7.1 %collective-permute-start.1 = (bf16[8,1,16,256]{3,2,1,0:T(8,128)(2,1)S(1)}, bf16[8,1,16,256]{3,2,1,0:T(8,128)(2,1)S(1)}, u32[]{:S(2)}, u32[]{:S(2)}) collective-permute-start(bf16[8,1,16,256]{3,2,1,0:T(8,128)(2,1)S(1)} %get-tuple-element.65), channel_id=1, source_target_pairs={{16,0},{32,16},{48,32},{64,48},{80,64},{96,80},{112,96},{17,1},{33... | collective-permute-start | bytes 196616 | tf_op jit(solution)/shard_map/ppermute | solution.py:18
  32.0 3.5 collective-permute-start.2
  33.3 5.4 %collective-permute-start.3 = (bf16[8,18,1,256]{3,2,1,0:T(2,128)(2,1)S(1)}, bf16[8,18,1,256]{3,2,1,0:T(2,128)(2,1)S(1)}, u32[]{:S(2)}, u32[]{:S(2)}) collective-permute-start(bf16[8,18,1,256]{3,2,1,0:T(2,128)(2,1)S(1)} %get-tuple-element.62), channel_id=1, source_target_pairs={{1,0},{2,1},{3,2},{4,3},{5,4},{6,5},{7,6},{8,7},{9,8},{10,9},{11,1... | collective-permute-start | bytes 221192 | tf_op jit(solution)/shard_map/ppermute | solution.py:18
  209.6 8.0 %collective-permute-start.4 = (bf16[8,4,4,1024]{3,0,2,1:T(8,128)(2,1)S(1)}, bf16[8,4,4,1024]{3,0,2,1:T(8,128)(2,1)S(1)}, u32[]{:S(2)}, u32[]{:S(2)}) collective-permute-start(bf16[8,4,4,1024]{3,0,2,1:T(8,128)(2,1)S(1)} %fusion.20), channel_id=1, source_target_pairs={{0,128},{128,0},{1,129},{129,1},{2,130},{130,2},{3,131},{131,3},{4... | collective-permute-start | bytes 786440 | tf_op jit(solution)/shard_map/ppermute | solution.py:26
  217.7 13.4 %copy-start.8 = (f32[1024]{0:T(1024)S(1)}, f32[1024]{0:T(1024)}, u32[]{:S(2)}) copy-start(f32[1024]{0:T(1024)} %param.18) | copy-start | bytes 12292
  230.1 50.6 %copy-start.4 = (bf16[3,1024,64]{1,2,0:T(8,128)(2,1)S(1)}, bf16[3,1024,64]{1,2,0:T(8,128)(2,1)}, u32[]{:S(2)}) copy-start(bf16[3,1024,64]{1,2,0:T(8,128)(2,1)} %param.19) | copy-start | bytes 1179652
  232.0 130.1 %reduce-scatter.3.cloned.1.call-start = ((), (), s32[]{:S(2)}) async-start(), calls=%async_computation.5 | async-start | bytes 4456448 | tf_op jit(solution)/shard_map/reduce_scatter | solution.py:124
  285.5 11.4 %copy-start.5 = (bf16[64,1024]{1,0:T(8,128)(2,1)S(1)}, bf16[64,1024]{1,0:T(8,128)(2,1)}, u32[]{:S(2)}) copy-start(bf16[64,1024]{1,0:T(8,128)(2,1)} %param.20) | copy-start | bytes 393220
  300.1 64.2 %copy-start.9 = (f32[1024]{0:T(1024)S(1)}, f32[1024]{0:T(1024)}, u32[]{:S(2)}) copy-start(f32[1024]{0:T(1024)} %param.21) | copy-start | bytes 12292
  300.2 106.8 %copy-start.10 = (bf16[1024,256]{1,0:T(8,128)(2,1)S(1)}, bf16[1024,256]{1,0:T(8,128)(2,1)}, u32[]{:S(2)}) copy-start(bf16[1024,256]{1,0:T(8,128)(2,1)} %param.22) | copy-start | bytes 1572868
  300.2 106.8 %all-gather.5.cloned.1.call-start = ((), (), s32[]{:S(2)}) async-start(), calls=%async_computation.6 | async-start | bytes 4456448 | tf_op jit(solution)/shard_map/all_gather | solution.py:133
  366.2 111.2 %reduce-scatter.5.cloned.1.call-start = ((), (), s32[]{:S(2)}) async-start(), calls=%async_computation.7 | async-start | bytes 4456448 | tf_op jit(solution)/shard_map/reduce_scatter | solution.py:142
  415.5 62.0 %copy-start.1 = (bf16[128,1024]{1,0:T(8,128)(2,1)S(1)}, bf16[128,1024]{1,0:T(8,128)(2,1)}, u32[]{:S(2)}) copy-start(bf16[128,1024]{1,0:T(8,128)(2,1)} %reduce-scatter.3.cloned.1.call-done) | copy-start | bytes 786436
Sparse Core Ops, SparseCore 0:
  232.2 48.5 all-gather.2
  300.3 61.7 reduce-scatter.2
  366.3 40.6 all-gather.4
  415.6 61.7 reduce-scatter.4
